TPU v7x, 256 devices: a 2x2x32 block of a 4x8x32 slice. The times are simulated.
256 devices in a mesh: groups: 4 (over x, y), rows: 64 (over z, core).
Axes of the slice: x: 2, y: 2, z: 32, core: 2. Of those that a mesh axis runs over, the one named last changes fastest.
The devices are a block of a 4x8x32 slice.
Arguments:
- phase: float32 [4096, 2048], P(('groups', 'rows')), parts along dimension 0, may hold values from -3.140625 to 3.140625
Outputs:
- filtered: float32 [2, 4096, 2048], P(None, ('groups', 'rows')), parts along dimension 1
- profile: float32 [12, 16], P('groups'), parts along dimension 0
There are 4 independent parts, one for each index of `groups`. A program takes and returns all parts, laid end to end along the dimension named above; each array names one. Nothing has to cross between parts.
All inputs are finite; a program needn't handle non-finite values.
Results may differ from a plain program's by a relative error of at most 0.00012.
Values sent between devices are 32-bit elements; how exact they have to be, the bound alone decides.
A program may use at most 64 MiB of HBM per device.

v0:
```python
import math

import jax
import jax.numpy as jnp
from jax import lax
from jax.sharding import PartitionSpec as P

ITERS = 3


EPS = 1e-06
PRECISE = lax.Precision.HIGHEST


def passed_along(block, axis, distance):
    devices = range(lax.axis_size(axis))
    route = [(i - distance, i) for i in devices if i - distance in devices]
    return lax.ppermute(block, axis, route)


def from_everyone(array, axis):
    length = lax.axis_size(axis)
    return lax.all_to_all(
        jnp.broadcast_to(array[None], (length, *array.shape)), axis, 0, 0, tiled=True
    )


def over_copies(array, axis):
    return from_everyone(array, axis).sum(axis=0)


def tables():
    counter = jnp.arange(32, dtype=jnp.int32)
    product = (counter[:, None] * counter[None, :] % 32).astype(jnp.float32)
    angles = product * (2.0 * math.pi / 32.0)
    offsets = jnp.arange(32, dtype=jnp.float32)
    ramp = 1.0 - jnp.abs(offsets - 15.5) / 16.0
    return (jnp.cos(angles), jnp.sin(angles), ramp)


def transform(real_part, imag_part, cos_table, sin_table, form):

    def apply(table, data):
        return jnp.einsum(form, table, data, precision=PRECISE)

    return (
        apply(cos_table, real_part) - apply(sin_table, imag_part),
        apply(cos_table, imag_part) + apply(sin_table, real_part),
    )


def filter_slab(extended, window_rows, first_weight):
    height = extended.shape[1]
    width = extended.shape[2]
    padded = jnp.pad(extended, ((0, 0), (0, 0), (0, 16)))
    blocks = padded.reshape(2, height // 16, 16, width // 16 + 1, 16).transpose(0, 2, 4, 1, 3)
    tall = jnp.concatenate([blocks[:, :, :, :-1], blocks[:, :, :, 1:]], axis=1)
    windows = jnp.concatenate([tall[..., :-1], tall[..., 1:]], axis=2)
    cos_table, sin_table, ramp = tables()
    real_part, imag_part = transform(windows[0], windows[1], cos_table, -sin_table, "kt,tsab->ksab")
    real_part, imag_part = transform(real_part, imag_part, cos_table, -sin_table, "ls,ksab->klab")
    power = real_part * real_part + imag_part * imag_part
    average = jnp.mean(power, axis=(0, 1), keepdims=True)
    factor = (power / (average + EPS)) ** 0.25
    real_part = factor * real_part
    imag_part = factor * imag_part
    real_part, imag_part = transform(
        real_part, imag_part, cos_table / 32.0, sin_table / 32.0, "kt,tsab->ksab"
    )
    real_part, imag_part = transform(
        real_part, imag_part, cos_table / 32.0, sin_table / 32.0, "ls,ksab->klab"
    )
    keep_rows = jnp.concatenate([first_weight[None], jnp.ones((window_rows - 1,), jnp.float32)])
    taper = ramp[:, None, None, None] * ramp[None, :, None, None] * keep_rows[None, None, :, None]
    results = jnp.stack([real_part * taper, imag_part * taper])
    righty = jnp.pad(results[:, :, 16:], ((0, 0), (0, 0), (0, 0), (0, 0), (1, 0)))[..., :-1]
    columns = results[:, :, :16] + righty
    upper = jnp.pad(columns[:, :16], ((0, 0), (0, 0), (0, 0), (0, 1), (0, 0)))
    lower = jnp.pad(columns[:, 16:], ((0, 0), (0, 0), (0, 0), (1, 0), (0, 0)))
    joined = upper + lower
    return joined.transpose(0, 3, 1, 4, 2).reshape(2, 16 * (window_rows + 1), width)


def residue_sums(slab_rows):
    padded = jnp.pad(slab_rows, ((0, 0), (0, 0), (0, 1)))
    first = padded[:, :-1, :-1]
    second = padded[:, :-1, 1:]
    third = padded[:, 1:, 1:]
    fourth = padded[:, 1:, :-1]

    def cross(left, right):
        return left[1] * right[0] - left[0] * right[1]

    loop = cross(first, second) + cross(second, third) + cross(third, fourth) + cross(fourth, first)
    height = loop.shape[0]
    width = loop.shape[1]
    return jnp.sum((loop * loop).reshape(height, width // 128, 128), axis=(0, 2))


def per_device(phase):
    slab_height = phase.shape[0]
    total_rows = slab_height * lax.axis_size("rows")
    field = jnp.stack([jnp.cos(phase), jnp.sin(phase)])
    locals_list = []
    for step in range(ITERS):
        below = passed_along(field, "rows", -1)
        extended = jnp.concatenate([field, below], axis=1)
        local_sums = residue_sums(extended[:, : slab_height + 1])
        summed = filter_slab(extended, slab_height // 16, jnp.ones((), jnp.float32))
        spill = passed_along(summed[:, slab_height:], "rows", 1)
        field = jnp.concatenate([summed[:, :16] + spill, summed[:, 16:slab_height]], axis=1)
        locals_list.append(local_sums)
    totals = over_copies(jnp.stack(locals_list), "rows")
    return (field, totals / (total_rows * 128.0))


def solution(mesh):
    return jax.shard_map(
        per_device,
        mesh=mesh,
        in_specs=(P(("groups", "rows"), None),),
        out_specs=(P(None, ("groups", "rows"), None), P("groups", None)),
        check_vma=False,
    )
```

profile of v0, /device:TPU:37, one launch (start us, length us, event | category | flops | bytes accessed | tf_op | source)
XLA Modules:
  0.0 174.2 jit_solution(4385575740458112864)
XLA Ops:
  0.6 1.4 cosine_bitcast_fusion
  2.0 22.4 %collective-permute-start = (f32[2,16,2048]{2,1,0:T(8,128)S(1)}, f32[2,16,2048]{2,1,0:T(8,128)S(1)}, u32[]{:S(2)}, u32[]{:S(2)}) collective-permute-start(f32[2,16,2048]{2,1,0:T(8,128)S(1)} %pad_maximum_fusion.6), channel_id=1, source_target_pairs={{1,0},{2,1},{3,2},{4,3},{5,4},{6,5},{7,6},{8,7},{9,8},{10,9},{11,1... | collective-permute-start | bytes 786440 | tf_op jit(solution)/shard_map/ppermute | solution.py:18
  24.5 1.1 collective-permute-done
  25.6 2.7 %reshape.314 = f32[2,2,16,129,16]{4,3,2,1,0:T(8,128)} reshape(f32[2,32,2064]{2,1,0:T(8,128)S(1)} %pad.50) | data formatting | bytes 1056768 | tf_op jit(solution)/shard_map/reshape | solution.py:56
  28.3 4.2 %copy.123 = f32[2,2,16,129,16]{3,2,4,1,0:T(8,128)S(1)} copy(f32[2,2,16,129,16]{4,3,2,1,0:T(8,128)} %reshape.314) | data formatting | bytes 1056768 | tf_op jit(solution)/shard_map/reshape | solution.py:56
  34.9 0.9 fusion.93
  36.5 0.9 fusion.97
  37.4 0.9 fusion.11
  38.4 1.0 fusion.101
  39.7 0.9 fusion.87
  40.6 0.9 fusion.91
  41.5 0.9 convolution_add_fusion.9
  42.4 0.9 convolution_subtract_fusion.9
  43.3 0.9 fusion.85
  44.2 1.4 fusion.81
  45.6 1.0 fusion.13
  46.6 1.0 fusion.15
  47.9 2.6 %copy.136 = f32[2,2,16,128,16]{4,3,2,1,0:T(8,128)} copy(f32[2,2,16,128,16]{3,4,2,1,0:T(8,128)S(1)} %add_bitcast_fusion.2) | data formatting | bytes 1048576 | tf_op jit(solution)/shard_map/transpose | solution.py:81
  50.5 4.7 %reshape.319 = f32[2,32,2048]{2,1,0:T(8,128)S(1)} reshape(f32[2,2,16,128,16]{4,3,2,1,0:T(8,128)} %copy.136) | data formatting | bytes 1048576 | tf_op jit(solution)/shard_map/reshape | solution.py:81
  55.2 2.0 %collective-permute-start.1 = (f32[2,16,2048]{2,1,0:T(8,128)S(1)}, f32[2,16,2048]{2,1,0:T(8,128)S(1)}, u32[]{:S(2)}, u32[]{:S(2)}) collective-permute-start(f32[2,16,2048]{2,1,0:T(8,128)S(1)} %slice.353), channel_id=1, source_target_pairs={{0,1},{1,2},{2,3},{3,4},{4,5},{5,6},{6,7},{7,8},{8,9},{9,10},{10,1... | collective-permute-start | bytes 786440 | tf_op jit(solution)/shard_map/ppermute | solution.py:18
  57.1 3.3 %collective-permute-done.1 = f32[2,16,2048]{2,1,0:T(8,128)S(1)} collective-permute-done((f32[2,16,2048]{2,1,0:T(8,128)S(1)}, f32[2,16,2048]{2,1,0:T(8,128)S(1)}, u32[]{:S(2)}, u32[]{:S(2)}) %collective-permute-start.1) | collective-permute-done | bytes 262176 | tf_op jit(solution)/shard_map/ppermute | solution.py:18
  60.5 2.0 %collective-permute-start.2 = (f32[2,16,2048]{2,1,0:T(8,128)S(1)}, f32[2,16,2048]{2,1,0:T(8,128)S(1)}, u32[]{:S(2)}, u32[]{:S(2)}) collective-permute-start(f32[2,16,2048]{2,1,0:T(8,128)S(1)} %slice_add_fusion.2), channel_id=1, source_target_pairs={{1,0},{2,1},{3,2},{4,3},{5,4},{6,5},{7,6},{8,7},{9,8},{10,9},{11,1... | collective-permute-start | bytes 786440 | tf_op jit(solution)/shard_map/ppermute | solution.py:18
  62.4 6.5 %collective-permute-done.2 = f32[2,16,2048]{2,1,0:T(8,128)S(1)} collective-permute-done((f32[2,16,2048]{2,1,0:T(8,128)S(1)}, f32[2,16,2048]{2,1,0:T(8,128)S(1)}, u32[]{:S(2)}, u32[]{:S(2)}) %collective-permute-start.2) | collective-permute-done | bytes 262176 | tf_op jit(solution)/shard_map/ppermute | solution.py:18
  69.0 2.7 %reshape.320 = f32[2,2,16,129,16]{4,3,2,1,0:T(8,128)} reshape(f32[2,32,2064]{2,1,0:T(8,128)S(1)} %pad.54) | data formatting | bytes 1056768 | tf_op jit(solution)/shard_map/reshape | solution.py:56
  71.7 4.0 %copy.137 = f32[2,2,16,129,16]{3,2,4,1,0:T(8,128)S(1)} copy(f32[2,2,16,129,16]{4,3,2,1,0:T(8,128)} %reshape.320) | data formatting | bytes 1056768 | tf_op jit(solution)/shard_map/reshape | solution.py:56
  78.1 0.9 fusion.75
  79.7 0.9 fusion.79
  80.7 0.9 fusion.7
  81.6 1.0 fusion.102
  82.9 0.9 fusion.69
  83.8 0.9 fusion.73
  84.7 0.9 convolution_add_fusion.5
  85.6 0.9 convolution_subtract_fusion.5
  86.5 0.9 fusion.67
  87.4 1.1 fusion.63
  88.6 1.0 fusion.17
  89.6 1.0 fusion.19
  90.8 2.6 %copy.150 = f32[2,2,16,128,16]{4,3,2,1,0:T(8,128)} copy(f32[2,2,16,128,16]{3,4,2,1,0:T(8,128)S(1)} %add_bitcast_fusion.1) | data formatting | bytes 1048576 | tf_op jit(solution)/shard_map/transpose | solution.py:81
  93.4 4.7 %reshape.325 = f32[2,32,2048]{2,1,0:T(8,128)S(1)} reshape(f32[2,2,16,128,16]{4,3,2,1,0:T(8,128)} %copy.150) | data formatting | bytes 1048576 | tf_op jit(solution)/shard_map/reshape | solution.py:81
  98.2 2.0 %collective-permute-start.3 = (f32[2,16,2048]{2,1,0:T(8,128)S(1)}, f32[2,16,2048]{2,1,0:T(8,128)S(1)}, u32[]{:S(2)}, u32[]{:S(2)}) collective-permute-start(f32[2,16,2048]{2,1,0:T(8,128)S(1)} %slice.365), channel_id=1, source_target_pairs={{0,1},{1,2},{2,3},{3,4},{4,5},{5,6},{6,7},{7,8},{8,9},{9,10},{10,1... | collective-permute-start | bytes 786440 | tf_op jit(solution)/shard_map/ppermute | solution.py:18
  100.9 2.5 %collective-permute-done.3 = f32[2,16,2048]{2,1,0:T(8,128)S(1)} collective-permute-done((f32[2,16,2048]{2,1,0:T(8,128)S(1)}, f32[2,16,2048]{2,1,0:T(8,128)S(1)}, u32[]{:S(2)}, u32[]{:S(2)}) %collective-permute-start.3) | collective-permute-done | bytes 262176 | tf_op jit(solution)/shard_map/ppermute | solution.py:18
  103.4 2.0 %collective-permute-start.4 = (f32[2,16,2048]{2,1,0:T(8,128)S(1)}, f32[2,16,2048]{2,1,0:T(8,128)S(1)}, u32[]{:S(2)}, u32[]{:S(2)}) collective-permute-start(f32[2,16,2048]{2,1,0:T(8,128)S(1)} %slice_add_fusion.1), channel_id=1, source_target_pairs={{1,0},{2,1},{3,2},{4,3},{5,4},{6,5},{7,6},{8,7},{9,8},{10,9},{11,1... | collective-permute-start | bytes 786440 | tf_op jit(solution)/shard_map/ppermute | solution.py:18
  105.8 6.1 %collective-permute-done.4 = f32[2,16,2048]{2,1,0:T(8,128)S(1)} collective-permute-done((f32[2,16,2048]{2,1,0:T(8,128)S(1)}, f32[2,16,2048]{2,1,0:T(8,128)S(1)}, u32[]{:S(2)}, u32[]{:S(2)}) %collective-permute-start.4) | collective-permute-done | bytes 262176 | tf_op jit(solution)/shard_map/ppermute | solution.py:18
  112.0 2.7 %reshape.326 = f32[2,2,16,129,16]{4,3,2,1,0:T(8,128)} reshape(f32[2,32,2064]{2,1,0:T(8,128)S(1)} %pad.58) | data formatting | bytes 1056768 | tf_op jit(solution)/shard_map/reshape | solution.py:56
  114.7 4.0 %copy.151 = f32[2,2,16,129,16]{3,2,4,1,0:T(8,128)S(1)} copy(f32[2,2,16,129,16]{4,3,2,1,0:T(8,128)} %reshape.326) | data formatting | bytes 1056768 | tf_op jit(solution)/shard_map/reshape | solution.py:56
  120.8 0.7 broadcast_in_dim.2
  121.5 21.2 %all-to-all-start = ((f32[64,3,16]{2,1,0:T(4,128)}), f32[64,3,16]{2,1,0:T(4,128)S(1)}, u32[]{:S(2)}, u32[]{:S(2)}) async-start(f32[64,3,16]{2,1,0:T(4,128)} %broadcast_in_dim.2), calls=%async_computation | async-start | bytes 262144 | tf_op jit(solution)/shard_map/all_to_all | solution.py:23
  143.3 0.9 fusion.57
  144.9 0.9 fusion.61
  145.9 1.0 fusion.3
  146.8 1.0 fusion.103
  148.1 0.9 fusion.51
  149.0 0.9 fusion.55
  149.9 0.9 convolution_add_fusion.1
  150.8 0.9 convolution_subtract_fusion.1
  151.7 0.9 fusion.49
  152.7 0.9 fusion.45
  153.6 1.0 fusion.21
  154.6 1.2 fusion.23
  156.1 2.6 %copy.164 = f32[2,2,16,128,16]{4,3,2,1,0:T(8,128)} copy(f32[2,2,16,128,16]{3,4,2,1,0:T(8,128)S(1)} %add_bitcast_fusion) | data formatting | bytes 1048576 | tf_op jit(solution)/shard_map/transpose | solution.py:81
  158.7 4.7 %reshape.331 = f32[2,32,2048]{2,1,0:T(8,128)S(1)} reshape(f32[2,2,16,128,16]{4,3,2,1,0:T(8,128)} %copy.164) | data formatting | bytes 1048576 | tf_op jit(solution)/shard_map/reshape | solution.py:81
  163.4 3.6 %collective-permute-start.5 = (f32[2,16,2048]{2,1,0:T(8,128)S(1)}, f32[2,16,2048]{2,1,0:T(8,128)S(1)}, u32[]{:S(2)}, u32[]{:S(2)}) collective-permute-start(f32[2,16,2048]{2,1,0:T(8,128)S(1)} %slice.377), channel_id=1, source_target_pairs={{0,1},{1,2},{2,3},{3,4},{4,5},{5,6},{6,7},{7,8},{8,9},{9,10},{10,1... | collective-permute-start | bytes 786440 | tf_op jit(solution)/shard_map/ppermute | solution.py:18
  167.0 5.5 %all-to-all-done = f32[64,3,16]{2,1,0:T(4,128)S(1)} async-done(((f32[64,3,16]{2,1,0:T(4,128)}), f32[64,3,16]{2,1,0:T(4,128)S(1)}, u32[]{:S(2)}, u32[]{:S(2)}) %all-to-all-start) | async-done | bytes 12320 | tf_op jit(solution)/shard_map/all_to_all | solution.py:23
  173.2 0.7 slice_add_fusion
  (65 shorter events, 13.1 us)
Async XLA Ops:
  2.0 23.5 %collective-permute-start = (f32[2,16,2048]{2,1,0:T(8,128)S(1)}, f32[2,16,2048]{2,1,0:T(8,128)S(1)}, u32[]{:S(2)}, u32[]{:S(2)}) collective-permute-start(f32[2,16,2048]{2,1,0:T(8,128)S(1)} %pad_maximum_fusion.6), channel_id=1, source_target_pairs={{1,0},{2,1},{3,2},{4,3},{5,4},{6,5},{7,6},{8,7},{9,8},{10,9},{11,1... | collective-permute-start | bytes 786440 | tf_op jit(solution)/shard_map/ppermute | solution.py:18
  55.2 5.3 %collective-permute-start.1 = (f32[2,16,2048]{2,1,0:T(8,128)S(1)}, f32[2,16,2048]{2,1,0:T(8,128)S(1)}, u32[]{:S(2)}, u32[]{:S(2)}) collective-permute-start(f32[2,16,2048]{2,1,0:T(8,128)S(1)} %slice.353), channel_id=1, source_target_pairs={{0,1},{1,2},{2,3},{3,4},{4,5},{5,6},{6,7},{7,8},{8,9},{9,10},{10,1... | collective-permute-start | bytes 786440 | tf_op jit(solution)/shard_map/ppermute | solution.py:18
  60.5 8.5 %collective-permute-start.2 = (f32[2,16,2048]{2,1,0:T(8,128)S(1)}, f32[2,16,2048]{2,1,0:T(8,128)S(1)}, u32[]{:S(2)}, u32[]{:S(2)}) collective-permute-start(f32[2,16,2048]{2,1,0:T(8,128)S(1)} %slice_add_fusion.2), channel_id=1, source_target_pairs={{1,0},{2,1},{3,2},{4,3},{5,4},{6,5},{7,6},{8,7},{9,8},{10,9},{11,1... | collective-permute-start | bytes 786440 | tf_op jit(solution)/shard_map/ppermute | solution.py:18
  90.8 9.3 %copy-start = (f32[16,2048]{1,0:T(8,128)S(1)}, f32[16,2048]{1,0:T(8,128)}, u32[]{:S(2)}) copy-start(f32[16,2048]{1,0:T(8,128)} %param.1) | copy-start | bytes 393220
  98.2 5.3 %collective-permute-start.3 = (f32[2,16,2048]{2,1,0:T(8,128)S(1)}, f32[2,16,2048]{2,1,0:T(8,128)S(1)}, u32[]{:S(2)}, u32[]{:S(2)}) collective-permute-start(f32[2,16,2048]{2,1,0:T(8,128)S(1)} %slice.365), channel_id=1, source_target_pairs={{0,1},{1,2},{2,3},{3,4},{4,5},{5,6},{6,7},{7,8},{8,9},{9,10},{10,1... | collective-permute-start | bytes 786440 | tf_op jit(solution)/shard_map/ppermute | solution.py:18
  103.4 8.5 %collective-permute-start.4 = (f32[2,16,2048]{2,1,0:T(8,128)S(1)}, f32[2,16,2048]{2,1,0:T(8,128)S(1)}, u32[]{:S(2)}, u32[]{:S(2)}) collective-permute-start(f32[2,16,2048]{2,1,0:T(8,128)S(1)} %slice_add_fusion.1), channel_id=1, source_target_pairs={{1,0},{2,1},{3,2},{4,3},{5,4},{6,5},{7,6},{8,7},{9,8},{10,9},{11,1... | collective-permute-start | bytes 786440 | tf_op jit(solution)/shard_map/ppermute | solution.py:18
  121.5 51.0 %all-to-all-start = ((f32[64,3,16]{2,1,0:T(4,128)}), f32[64,3,16]{2,1,0:T(4,128)S(1)}, u32[]{:S(2)}, u32[]{:S(2)}) async-start(f32[64,3,16]{2,1,0:T(4,128)} %broadcast_in_dim.2), calls=%async_computation | async-start | bytes 262144 | tf_op jit(solution)/shard_map/all_to_all | solution.py:23
  163.4 9.7 %collective-permute-start.5 = (f32[2,16,2048]{2,1,0:T(8,128)S(1)}, f32[2,16,2048]{2,1,0:T(8,128)S(1)}, u32[]{:S(2)}, u32[]{:S(2)}) collective-permute-start(f32[2,16,2048]{2,1,0:T(8,128)S(1)} %slice.377), channel_id=1, source_target_pairs={{0,1},{1,2},{2,3},{3,4},{4,5},{5,6},{6,7},{7,8},{8,9},{9,10},{10,1... | collective-permute-start | bytes 786440 | tf_op jit(solution)/shard_map/ppermute | solution.py:18
where the time goes:
time: 177 us; the launch traced here: 174 us
  starting transfers between devices  54.9 us (31%)
  local copies, waits for them, and re-layouts  44.9 us (25%)
  matrix products  42.3 us (24%)
  waiting for transfers between devices  25 us (14%)
  other arithmetic  5.47 us (3%)
    dot_general x48, matrix products, apply(): return jnp.einsum(form, table, data, precision=PRECISE)  42.3 us
    ppermute x6, starting transfers between devices, passed_along(): return lax.ppermute(block, axis, route)  33.7 us
    all_to_all x1, starting transfers between devices, from_everyone(): lax.all_to_all(jnp.broadcast_to(array[None], (length, *array.shape)), axi...  21.2 us
    reshape x6, local copies, waits for them, and re-layouts, filter_slab(): padded.reshape(2, height // 16, 16, width // 16 + 1, 16)  20.4 us
    ppermute x6, waiting for transfers between devices, passed_along(): return lax.ppermute(block, axis, route)  19.5 us
    reshape x3, local copies, waits for them, and re-layouts, filter_slab(): joined.transpose(0, 3, 1, 4, 2).reshape(2, 16 * (window_rows + 1), width)  14.1 us
    transpose x3, local copies, waits for them, and re-layouts, filter_slab(): joined.transpose(0, 3, 1, 4, 2).reshape(2, 16 * (window_rows + 1), width)  7.79 us
    all_to_all x1, waiting for transfers between devices, from_everyone(): lax.all_to_all(jnp.broadcast_to(array[None], (length, *array.shape)), axi...  5.49 us
  transfers between devices with their start and end apart: 7, of which 6 were waited for; matrix products, arithmetic and copies ran while one was open for 13% of the time, Pallas kernels for 0%

commit v1 on v0

v1 whole, which is shorter than its diff:
```python
import functools
import math

import jax
import jax.numpy as jnp
import numpy as np
from jax import lax
from jax.experimental import pallas as pl
from jax.experimental.pallas import tpu as pltpu
from jax.sharding import PartitionSpec as P

ITERS = 3
EPS = 1e-06
WIN = 32
HALF = 16
LANES = 128
F32 = jnp.float32
BF16 = jnp.bfloat16
MESH = pl.DeviceIdType.MESH

PHASE_ENDS = (7, 12, 16)
CHUNK_ENDS = ((6, 11, 16), (5, 10, 16), (4, 9, 16))


def hi_lo(table):
    high = table.astype(np.float32).astype(jnp.bfloat16)
    low = (table - high.astype(np.float64)).astype(np.float32).astype(jnp.bfloat16)
    return high, low


def tables():
    counter = np.arange(WIN)
    angles = 2.0 * math.pi / WIN * (counter[:, None] * counter[None, :] % WIN)
    cos, sin = np.cos(angles), np.sin(angles)
    ramp = 1.0 - np.abs(counter - 15.5) / 16.0

    def rows(real, imag):
        return np.concatenate([real[:HALF], imag[:HALF], real[HALF:], imag[HALF:]])

    forward = np.concatenate(
        [rows(cos.T, sin.T).T, rows(-sin.T, cos.T).T], axis=0
    )
    high, low = hi_lo(forward)
    row_in = np.concatenate([high, high, low], axis=1)
    scale = ramp[:, None] / WIN
    backward = rows(
        np.concatenate([cos, -sin], axis=1) * scale, np.concatenate([sin, cos], axis=1) * scale
    )
    high, low = hi_lo(backward)
    row_out = np.concatenate([high, high, low], axis=1)
    four = np.eye(LANES // WIN)
    c, s = np.kron(four, cos), np.kron(four, sin)
    high, low = hi_lo(np.block([[c, -s], [s, c]]))
    col_in = np.concatenate([high, high, low], axis=0)
    taper = np.tile(ramp, LANES // WIN)[None, :] / WIN
    high, low = hi_lo(np.block([[c * taper, s * taper], [-s * taper, c * taper]]))
    col_out = np.concatenate([high, high, low], axis=0)
    ones = np.kron(four, np.ones((WIN, WIN)))
    ones = np.concatenate([ones, ones], axis=0).astype(jnp.bfloat16)
    return [row_in, col_in, col_out, row_out, ones]


def split(x):
    high = x.astype(BF16)
    return high, (x - high.astype(F32)).astype(BF16)


def split_rows(x):
    high, low = split(x)
    return jnp.concatenate([high, low, high], axis=0)


def split_cols(x):
    high, low = split(x)
    return jnp.concatenate([high, low, high], axis=1)


def dot(a, b):
    return jnp.dot(a, b, preferred_element_type=F32)


def unit(phase):
    y = phase * 0.5
    t = y * y
    sine = -1.0 / 39916800.0
    for c in (1.0 / 362880.0, -1.0 / 5040.0, 1.0 / 120.0, -1.0 / 6.0, 1.0):
        sine = sine * t + c
    sine = sine * y
    cosine = 1.0 / 479001600.0
    for c in (-1.0 / 3628800.0, 1.0 / 40320.0, -1.0 / 720.0, 1.0 / 24.0, -0.5, 1.0):
        cosine = cosine * t + c
    return 1.0 - 2.0 * (sine * sine), 2.0 * (sine * cosine)


def to_lanes(tiles):
    return jnp.concatenate([tiles[j] for j in range(tiles.shape[0])], axis=1)


def to_tiles(wide):
    return jnp.stack(
        [wide[:, LANES * j : LANES * (j + 1)] for j in range(wide.shape[1] // LANES)]
    )


def kernel(
    n,
    tiles,
    phase_hbm,
    row_in_hbm,
    col_in_hbm,
    col_out_hbm,
    row_out_hbm,
    ones_hbm,
    out_hbm,
    prof_ref,
    phase,
    row_in,
    col_in,
    col_out,
    row_out,
    ones,
    x,
    eo,
    rv,
    carry,
    zout,
    pay_a,
    pay_b,
    got_a,
    got_b,
    load_sem,
    ph_send,
    ph_recv,
    up_send,
    up_recv,
    dn_send,
    dn_recv,
    a_send,
    a_recv,
    b_send,
    b_recv,
    out_sem,
    relay,
):
    me = lax.axis_index("rows")
    has_above = me > 0
    has_below = me < n - 1

    def ring(offset):
        return {"rows": lax.rem(me + (offset + n), n)}

    def greet(sem, distance):
        for offset in (-distance, distance):
            pl.semaphore_signal(sem, inc=1, device_id=ring(offset), device_id_type=MESH)

    barrier = pltpu.get_barrier_semaphore()
    greet(barrier, 1)

    loads = [
        pltpu.make_async_copy(src, dst, load_sem.at[i])
        for i, (src, dst) in enumerate(
            [
                (phase_hbm, phase.at[0]),
                (row_in_hbm, row_in),
                (ones_hbm, ones),
                (col_in_hbm, col_in),
                (col_out_hbm, col_out),
                (row_out_hbm, row_out),
            ]
        )
    ]
    for load in loads:
        load.start()

    keep_below = jnp.where(has_below, 1.0, 0.0).astype(F32)

    @pl.when(jnp.logical_not(has_above))
    def _():
        rv[:, 0] = jnp.zeros(rv.shape[:1] + rv.shape[2:], F32)

    @pl.when(jnp.logical_not(has_below))
    def _():
        rv[:, 1] = jnp.zeros(rv.shape[:1] + rv.shape[2:], F32)
        phase[1] = jnp.zeros(phase.shape[1:], F32)

    x[tiles] = jnp.zeros(x.shape[1:], F32)
    loads[0].wait()
    pl.semaphore_wait(barrier, 2)

    stages = relay.shape[0]
    greet(relay.at[0], 1)

    def relay_step(s):
        if s < stages:
            pl.semaphore_wait(relay.at[s], 2)
            if s + 1 < stages:
                greet(relay.at[s + 1], 2 ** (s + 1))

    def phase_copy(c):
        first = PHASE_ENDS[c - 1] if c else 0
        cols = pl.ds(first * LANES, (PHASE_ENDS[c] - first) * LANES)
        return pltpu.make_async_remote_copy(
            src_ref=phase.at[0, :, cols],
            dst_ref=phase.at[1, :, cols],
            send_sem=ph_send.at[c],
            recv_sem=ph_recv.at[c],
            device_id={"rows": jnp.maximum(me - 1, 0)},
            device_id_type=MESH,
        )

    def span(it, c):
        ends = CHUNK_ENDS[it]
        return (ends[c - 1] if c else 0), ends[c]

    def up_copy(it, c):
        lo, hi = span(it, c)
        return pltpu.make_async_remote_copy(
            src_ref=eo.at[it, 0, pl.ds(lo, hi - lo)],
            dst_ref=rv.at[it, 1, pl.ds(lo, hi - lo)],
            send_sem=up_send.at[it, c],
            recv_sem=up_recv.at[it, c],
            device_id={"rows": jnp.maximum(me - 1, 0)},
            device_id_type=MESH,
        )

    def dn_copy(it, c):
        lo, hi = span(it, c)
        return pltpu.make_async_remote_copy(
            src_ref=eo.at[it, 1, pl.ds(lo, hi - lo)],
            dst_ref=rv.at[it, 0, pl.ds(lo, hi - lo)],
            send_sem=dn_send.at[it, c],
            recv_sem=dn_recv.at[it, c],
            device_id={"rows": jnp.minimum(me + 1, n - 1)},
            device_id_type=MESH,
        )

    @pl.when(has_above)
    def _():
        for c in range(len(PHASE_ENDS)):
            phase_copy(c).start()

    lane = lax.broadcasted_iota(jnp.int32, (1, 1, LANES), 2)

    def unit_tiles(row, lo, hi, scale=None):
        real, imag = unit(phase[row, :, lo * LANES : hi * LANES])
        if scale is not None:
            real, imag = real * scale, imag * scale
        return to_tiles(jnp.concatenate([real, imag], axis=0))

    x[0:tiles, 0:WIN] = unit_tiles(0, 0, tiles)
    for load in loads[1:]:
        load.wait()
    below_rows = lax.broadcasted_iota(jnp.int32, row_out.shape, 0) >= WIN
    row_out[...] = jnp.where(
        jnp.logical_and(below_rows, jnp.logical_not(has_below)),
        jnp.zeros(row_out.shape, BF16),
        row_out[...],
    )

    def arrive(it, c):
        if it == 0:
            lo, hi = (PHASE_ENDS[c - 1] if c else 0), PHASE_ENDS[c]

            @pl.when(has_above)
            def _():
                phase_copy(c).wait_send()

            @pl.when(has_below)
            def _():
                phase_copy(c).wait_recv()

            x[lo:hi, WIN:] = unit_tiles(1, lo, hi, keep_below)
            return hi
        lo, hi = span(it - 1, c)

        @pl.when(has_above)
        def _():
            up_copy(it - 1, c).wait_send()
            dn_copy(it - 1, c).wait_recv()

        @pl.when(has_below)
        def _():
            up_copy(it - 1, c).wait_recv()
            dn_copy(it - 1, c).wait_send()

        x[lo:hi] = jnp.concatenate(
            [eo[it - 1, 0, lo:hi] + rv[it - 1, 0, lo:hi], eo[it - 1, 1, lo:hi] + rv[it - 1, 1, lo:hi]],
            axis=1,
        )
        return hi

    def residues(it, lo, hi):
        field = x[lo : hi + 1]
        last_row = lax.broadcasted_iota(jnp.int32, (1, HALF, 1), 1) == HALF - 1

        def lower(a, b):
            return jnp.where(last_row, b[:, 0:1], pltpu.roll(a, HALF - 1, 1))

        def right(a):
            return pltpu.roll(jnp.where(lane == 0, a[1:], a[:-1]), LANES - 1, 2)

        ar, ai = field[:, 0:HALF], field[:, HALF:WIN]
        dr = lower(ar, field[:, WIN : WIN + HALF])
        di = lower(ai, field[:, WIN + HALF :])
        pr, pi = ar[:-1] - right(dr), ai[:-1] - right(di)
        qr, qi = right(ar) - dr[:-1], right(ai) - di[:-1]
        loop = pi * qr - pr * qi
        loop = loop * loop
        loop = loop[:, 0:8] + loop[:, 8:HALF]
        sums = jnp.sum(loop, axis=2, keepdims=True)
        lanes = lax.broadcasted_iota(jnp.int32, (8, LANES), 1)
        total = jnp.zeros((8, LANES), F32)
        for j in range(hi - lo):
            total = jnp.where(lanes == it * tiles + lo + j, sums[j], total)
        return total

    def windows(it, lo, hi):
        count = hi - lo
        field = x[lo : hi + 1]
        y = to_tiles(dot(row_in[...], split_rows(to_lanes(field))))
        square = field * field
        square = sum(square[:, 8 * i : 8 * i + 8] for i in range(8))

        def both(tall):
            odd = pltpu.roll(jnp.where(lane < HALF, tall[1:], tall[:-1]), LANES - HALF, 2)
            return jnp.concatenate([tall[:-1], odd], axis=0)

        high, low = split(both(square).reshape(2 * count * 8, LANES))
        mean = dot(jnp.concatenate([high, low], axis=1), ones[...])
        mean = jnp.sum(mean.reshape(2 * count, 8, LANES), axis=1, keepdims=True)
        inverse = 1.0 / (mean + EPS)

        y = both(y)
        y = jnp.concatenate([y[:, 0:WIN], y[:, WIN:]], axis=2).reshape(2 * count * WIN, 2 * LANES)
        s = dot(split_cols(y), col_in[...]).reshape(2 * count, WIN, 2 * LANES)
        sr, si = s[:, :, 0:LANES], s[:, :, LANES:]
        gain = lax.rsqrt(lax.rsqrt((sr * sr + si * si) * inverse))
        s = jnp.concatenate([sr * gain, si * gain], axis=2).reshape(2 * count * WIN, 2 * LANES)
        s = dot(split_cols(s), col_out[...]).reshape(2 * count, WIN, 2 * LANES)
        s = jnp.concatenate([s[:, :, 0:LANES], s[:, :, LANES:]], axis=1)
        moved = pltpu.roll(s[count:], HALF, 2)
        if lo == 0:
            before = jnp.zeros((1, 2 * WIN, LANES), F32)
        else:
            before = carry[...][None]
        if hi < tiles:
            carry[...] = moved[count - 1]
        before = jnp.concatenate([before, moved[:-1]], axis=0)
        s = s[:count] + jnp.where(lane < HALF, before, moved)
        result = to_tiles(dot(row_out[...], split_rows(to_lanes(s))))
        eo[it, 0, lo:hi] = result[:, 0:WIN]
        eo[it, 1, lo:hi] = result[:, WIN:]

    group = a_send.shape[0] + 1
    a_offsets = [o for o in range(-(group // 2), group - group // 2) if o]
    b_offsets = [group * j for j in range(1, n // group)]

    def a_copy(i):
        return pltpu.make_async_remote_copy(
            src_ref=pay_a,
            dst_ref=got_a.at[i],
            send_sem=a_send.at[i],
            recv_sem=a_recv.at[i],
            device_id=ring(a_offsets[i]),
            device_id_type=MESH,
        )

    def b_copy(i):
        return pltpu.make_async_remote_copy(
            src_ref=pay_b,
            dst_ref=got_b.at[i],
            send_sem=b_send.at[i],
            recv_sem=b_recv.at[i],
            device_id=ring(b_offsets[i]),
            device_id_type=MESH,
        )

    chunks = len(PHASE_ENDS)
    payload = jnp.zeros((8, LANES), F32)
    done_stages = 0
    for it in range(ITERS):
        last = it == ITERS - 1
        if last:
            for c in range(chunks):
                arrive(it, c)
            payload = payload + residues(it, 0, tiles)
            pay_a[...] = jnp.sum(payload, axis=0, keepdims=True)
            for i in range(len(a_offsets)):
                a_copy(i).start()
        for c in range(chunks):
            lo, hi = span(it, c)
            if not last:
                arrive(it, c)
                payload = payload + residues(it, lo, hi)
            windows(it, lo, hi)
            if not last:

                @pl.when(has_above)
                def _():
                    up_copy(it, c).start()

            @pl.when(has_below)
            def _():
                dn_copy(it, c).start()

            if it * chunks + c < 4 and done_stages < stages:
                relay_step(done_stages)
                done_stages += 1
    while done_stages < stages:
        relay_step(done_stages)
        done_stages += 1

    total = pay_a[...]
    for i in range(len(a_offsets)):
        a_copy(i).wait()
        total = total + got_a[i]
    pay_b[...] = total
    for i in range(len(b_offsets)):
        b_copy(i).start()

    for c in range(chunks):
        lo, hi = span(ITERS - 1, c)

        @pl.when(has_above)
        def _():
            dn_copy(ITERS - 1, c).wait_recv()

        @pl.when(has_below)
        def _():
            dn_copy(ITERS - 1, c).wait_send()

        final = to_lanes(eo[ITERS - 1, 0, lo:hi] + rv[ITERS - 1, 0, lo:hi])
        zout[0, :, lo * LANES : hi * LANES] = final[0:HALF]
        zout[1, :, lo * LANES : hi * LANES] = final[HALF:]
    store = pltpu.make_async_copy(zout, out_hbm, out_sem)
    store.start()

    for i in range(len(b_offsets)):
        b_copy(i).wait()
        total = total + got_b[i]
    total = total * (1.0 / (n * HALF * LANES))
    for it in range(ITERS):
        moved = total if it == 0 else pltpu.roll(total, LANES - it * tiles, 1)
        prof_ref[it : it + 1, :] = moved[:, 0:tiles]
    store.wait()


def per_device(phase):
    n = lax.axis_size("rows")
    height, width = phase.shape
    tiles = width // LANES
    consts = [jnp.asarray(t) for t in tables()]
    stages = max(1, int(math.log2(n)) - 1)
    group = 8
    far = n // group - 1
    chunks = len(PHASE_ENDS)
    dma = pltpu.SemaphoreType.DMA
    any_spec = pl.BlockSpec(memory_space=pl.ANY)
    return pl.pallas_call(
        functools.partial(kernel, n, tiles),
        out_shape=(
            jax.ShapeDtypeStruct((2, height, width), F32),
            jax.ShapeDtypeStruct((ITERS, tiles), F32),
        ),
        in_specs=[any_spec] * 6,
        out_specs=(any_spec, pl.BlockSpec(memory_space=pltpu.VMEM)),
        scratch_shapes=[
            pltpu.VMEM((2, height, width), F32),
            *[pltpu.VMEM(c.shape, c.dtype) for c in consts[:4]],
            pltpu.VMEM(consts[4].shape, consts[4].dtype),
            pltpu.VMEM((tiles + 1, 2 * WIN, LANES), F32),
            pltpu.VMEM((ITERS, 2, tiles, WIN, LANES), F32),
            pltpu.VMEM((ITERS, 2, tiles, WIN, LANES), F32),
            pltpu.VMEM((2 * WIN, LANES), F32),
            pltpu.VMEM((2, height, width), F32),
            pltpu.VMEM((1, LANES), F32),
            pltpu.VMEM((1, LANES), F32),
            pltpu.VMEM((group - 1, 1, LANES), F32),
            pltpu.VMEM((far, 1, LANES), F32),
            dma((6,)),
            dma((chunks,)),
            dma((chunks,)),
            dma((ITERS, chunks)),
            dma((ITERS, chunks)),
            dma((ITERS, chunks)),
            dma((ITERS, chunks)),
            dma((group - 1,)),
            dma((group - 1,)),
            dma((far,)),
            dma((far,)),
            dma,
            pltpu.SemaphoreType.REGULAR((stages,)),
        ],
        compiler_params=pltpu.CompilerParams(
            collective_id=0, has_side_effects=True, vmem_limit_bytes=60 << 20
        ),
        name="goldstein",
    )(phase, *consts)


def solution(mesh):
    return jax.shard_map(
        per_device,
        mesh=mesh,
        in_specs=(P(("groups", "rows"), None),),
        out_specs=(P(None, ("groups", "rows"), None), P("groups", None)),
        check_vma=False,
    )
```

time: 177 us -> 59.1 us (0.33); the launches traced: 174 us -> 59 us
  Pallas kernels: 0 us -> 56.1 us
  starting transfers between devices: 54.9 us -> 0 us
  local copies, waits for them, and re-layouts: 44.9 us -> 2.25 us
  matrix products: 42.3 us -> 0 us
  waiting for transfers between devices: 25 us -> 0 us
  other arithmetic: 5.47 us -> 0 us
    pallas_call x0 -> x1, Pallas kernels: none -> 56.1 us  [per_device(): pl.pallas_call(functools.partial(kernel, n, tiles), out_shape=(jax.ShapeD...]
    dot_general x48 -> x0, matrix products: 42.3 us -> none  [apply(): return jnp.einsum(form, table, data, precision=PRECISE)]
    reshape x9 -> x0, local copies, waits for them, and re-layouts: 34.5 us -> none  [the longest x6 20.4 us: filter_slab(): padded.reshape(2, height // 16, 16, width // 16 + 1, 16)]
    ppermute x6 -> x0, starting transfers between devices: 33.7 us -> none  [passed_along(): return lax.ppermute(block, axis, route)]
    all_to_all x1 -> x0, starting transfers between devices: 21.2 us -> none  [from_everyone(): lax.all_to_all(jnp.broadcast_to(array[None], (length, *array.shape)), axi...]
    ppermute x6 -> x0, waiting for transfers between devices: 19.5 us -> none  [passed_along(): return lax.ppermute(block, axis, route)]
    transpose x3 -> x0, local copies, waits for them, and re-layouts: 7.79 us -> none  [filter_slab(): joined.transpose(0, 3, 1, 4, 2).reshape(2, 16 * (window_rows + 1), width)]
    all_to_all x1 -> x0, waiting for transfers between devices: 5.49 us -> none  [from_everyone(): lax.all_to_all(jnp.broadcast_to(array[None], (length, *array.shape)), axi...]
  transfers between devices with their start and end apart: 7 -> 0, of which waited for: 6 -> 0; matrix products, arithmetic and copies ran while one was open for 13% -> 0% of each run, Pallas kernels for 0% -> 0%
where the time goes in v1:
time: 59.1 us; the launch traced here: 59 us
  Pallas kernels  56.1 us (95%)
  local copies, waits for them, and re-layouts  2.25 us (4%)
  between operations  0.65 us (1%)
    pallas_call x1, Pallas kernels, per_device(): pl.pallas_call(functools.partial(kernel, n, tiles), out_shape=(jax.ShapeD...  56.1 us
    unnamed x4, local copies, waits for them, and re-layouts  2.25 us

profile of v1, /device:TPU:37, one launch (start us, length us, event | category | flops | bytes accessed | tf_op | source)
XLA Modules:
  0.0 59.0 jit_solution(7168138735037261510)
XLA Ops:
  0.6 56.1 %goldstein.1 = (f32[2,16,2048]{2,1,0:T(8,128)}, f32[3,16]{1,0:T(4,128)}) custom-call(f32[16,2048]{1,0:T(8,128)} %phase_hbm.1, bf16[64,192]{1,0:T(8,128)(2,1)} %constant.10.clone.row_in_hbm, bf16[768,256]{1,0:T(8,128)(2,1)} %constant.11.clone.col_in_hbm, bf16[768,256]{1,0:T(8,128)(2,1)} %constant.12.clone.col_out_hbm, ...), custom_call_target="tpu_custom_call" | custom-call | tf_op jit(solution)/shard_map/goldstein/pallas_call | solution.py:459
  56.7 0.0 copy-start
  56.7 1.7 %copy.10 = f32[2,16,2048]{2,1,0:T(8,128)} copy(f32[2,16,2048]{2,1,0:T(8,128)} %get-tuple-element.4) | data formatting | bytes 524288
  58.4 0.0 copy-done
  58.4 0.6 copy.11
Async XLA Ops:
  56.7 1.7 %copy-start = (f32[3,16]{1,0:T(4,128)S(1)}, f32[3,16]{1,0:T(4,128)}, u32[]{:S(2)}) copy-start(f32[3,16]{1,0:T(4,128)} %get-tuple-element.5) | copy-start | bytes 580

commit v2 on v1

--- a/solution.py
+++ b/solution.py
@@ -17,6 +17,7 @@
 F32 = jnp.float32
 BF16 = jnp.bfloat16
 MESH = pl.DeviceIdType.MESH
+ROOTS = 4
 
 PHASE_ENDS = (7, 12, 16)
 CHUNK_ENDS = ((6, 11, 16), (5, 10, 16), (4, 9, 16))
@@ -124,10 +125,9 @@
     rv,
     carry,
     zout,
-    pay_a,
-    pay_b,
-    got_a,
-    got_b,
+    pay,
+    got,
+    answer,
     load_sem,
     ph_send,
     ph_recv,
@@ -135,10 +135,10 @@
     up_recv,
     dn_send,
     dn_recv,
-    a_send,
-    a_recv,
-    b_send,
-    b_recv,
+    pay_send,
+    pay_recv,
+    ans_send,
+    ans_recv,
     out_sem,
     relay,
 ):
@@ -155,6 +155,7 @@
 
     barrier = pltpu.get_barrier_semaphore()
     greet(barrier, 1)
+    greet(barrier, 2)
 
     loads = [
         pltpu.make_async_copy(src, dst, load_sem.at[i])
@@ -185,16 +186,16 @@
 
     x[tiles] = jnp.zeros(x.shape[1:], F32)
     loads[0].wait()
-    pl.semaphore_wait(barrier, 2)
+    pl.semaphore_wait(barrier, 4)
 
     stages = relay.shape[0]
-    greet(relay.at[0], 1)
+    greet(relay.at[0], 2)
 
     def relay_step(s):
         if s < stages:
             pl.semaphore_wait(relay.at[s], 2)
             if s + 1 < stages:
-                greet(relay.at[s + 1], 2 ** (s + 1))
+                greet(relay.at[s + 1], 4 * 2 ** s)
 
     def phase_copy(c):
         first = PHASE_ENDS[c - 1] if c else 0
@@ -351,98 +352,153 @@
         eo[it, 0, lo:hi] = result[:, 0:WIN]
         eo[it, 1, lo:hi] = result[:, WIN:]
 
-    group = a_send.shape[0] + 1
-    a_offsets = [o for o in range(-(group // 2), group - group // 2) if o]
-    b_offsets = [group * j for j in range(1, n // group)]
-
-    def a_copy(i):
+    def pay_copy(root):
         return pltpu.make_async_remote_copy(
-            src_ref=pay_a,
-            dst_ref=got_a.at[i],
-            send_sem=a_send.at[i],
-            recv_sem=a_recv.at[i],
-            device_id=ring(a_offsets[i]),
+            src_ref=pay,
+            dst_ref=got.at[lax.rem(me - root + n, n)],
+            send_sem=pay_send.at[root],
+            recv_sem=pay_recv,
+            device_id={"rows": root},
             device_id_type=MESH,
         )
 
-    def b_copy(i):
+    def answer_copy(i):
         return pltpu.make_async_remote_copy(
-            src_ref=pay_b,
-            dst_ref=got_b.at[i],
-            send_sem=b_send.at[i],
-            recv_sem=b_recv.at[i],
-            device_id=ring(b_offsets[i]),
+            src_ref=answer,
+            dst_ref=answer,
+            send_sem=ans_send.at[i],
+            recv_sem=ans_recv,
+            device_id={"rows": jnp.minimum(me + ROOTS * (i + 1), n - 1)},
             device_id_type=MESH,
         )
 
     chunks = len(PHASE_ENDS)
     payload = jnp.zeros((8, LANES), F32)
-    done_stages = 0
-    for it in range(ITERS):
-        last = it == ITERS - 1
-        if last:
-            for c in range(chunks):
-                arrive(it, c)
-            payload = payload + residues(it, 0, tiles)
-            pay_a[...] = jnp.sum(payload, axis=0, keepdims=True)
-            for i in range(len(a_offsets)):
-                a_copy(i).start()
+    relay_step(0)
+    for it in range(ITERS - 1):
         for c in range(chunks):
             lo, hi = span(it, c)
-            if not last:
-                arrive(it, c)
-                payload = payload + residues(it, lo, hi)
+            arrive(it, c)
+            if c == 0 and it == 0:
+                relay_step(1)
             windows(it, lo, hi)
-            if not last:
-
-                @pl.when(has_above)
-                def _():
-                    up_copy(it, c).start()
+
+            @pl.when(has_above)
+            def _():
+                up_copy(it, c).start()
 
             @pl.when(has_below)
             def _():
                 dn_copy(it, c).start()
 
-            if it * chunks + c < 4 and done_stages < stages:
-                relay_step(done_stages)
-                done_stages += 1
-    while done_stages < stages:
-        relay_step(done_stages)
-        done_stages += 1
-
-    total = pay_a[...]
-    for i in range(len(a_offsets)):
-        a_copy(i).wait()
-        total = total + got_a[i]
-    pay_b[...] = total
-    for i in range(len(b_offsets)):
-        b_copy(i).start()
-
+        payload = payload + residues(it, 0, tiles)
+        if it == 0:
+            relay_step(2)
+
+    last = ITERS - 1
     for c in range(chunks):
-        lo, hi = span(ITERS - 1, c)
+        arrive(last, c)
+        payload = payload + residues(last, *span(last, c))
+    pay[...] = jnp.sum(payload, axis=0, keepdims=True)
+    for s in range(3, stages):
+        relay_step(s)
+    for root in range(ROOTS):
+
+        @pl.when(me != root)
+        def _():
+            pay_copy(root).start()
+
+    for c in range(chunks):
+        windows(last, *span(last, c))
+
+        @pl.when(has_below)
+        def _():
+            dn_copy(last, c).start()
+
+    for c in range(chunks):
+        lo, hi = span(last, c)
 
         @pl.when(has_above)
         def _():
-            dn_copy(ITERS - 1, c).wait_recv()
+            dn_copy(last, c).wait_recv()
 
         @pl.when(has_below)
         def _():
-            dn_copy(ITERS - 1, c).wait_send()
-
-        final = to_lanes(eo[ITERS - 1, 0, lo:hi] + rv[ITERS - 1, 0, lo:hi])
+            dn_copy(last, c).wait_send()
+
+        final = to_lanes(eo[last, 0, lo:hi] + rv[last, 0, lo:hi])
         zout[0, :, lo * LANES : hi * LANES] = final[0:HALF]
         zout[1, :, lo * LANES : hi * LANES] = final[HALF:]
     store = pltpu.make_async_copy(zout, out_hbm, out_sem)
     store.start()
-
-    for i in range(len(b_offsets)):
-        b_copy(i).wait()
-        total = total + got_b[i]
-    total = total * (1.0 / (n * HALF * LANES))
+    store.wait()
+    for root in range(ROOTS):
+
+        @pl.when(me != root)
+        def _():
+            pay_copy(root).wait_send()
+
+    is_root = me < ROOTS
+    answers = ans_send.shape[0]
+
+    @pl.when(is_root)
+    def _():
+        others = got.at[pl.ds(1, n - 1)]
+        pltpu.make_async_remote_copy(
+            src_ref=others,
+            dst_ref=others,
+            send_sem=pay_send.at[0],
+            recv_sem=pay_recv,
+            device_id=ring(1),
+            device_id_type=MESH,
+        ).wait_recv()
+        total = pay[...] + jnp.sum(got[1:n], axis=0)
+        answer[...] = total * (1.0 / (n * HALF * LANES))
+        for i in range(answers):
+            answer_copy(i).start()
+
+    @pl.when(jnp.logical_not(is_root))
+    def _():
+        answer_copy(0).wait_recv()
+
     for it in range(ITERS):
-        moved = total if it == 0 else pltpu.roll(total, LANES - it * tiles, 1)
+        moved = answer[...] if it == 0 else pltpu.roll(answer[...], LANES - it * tiles, 1)
         prof_ref[it : it + 1, :] = moved[:, 0:tiles]
-    store.wait()
+
+    @pl.when(is_root)
+    def _():
+        for i in range(answers):
+            answer_copy(i).wait_send()
+
+
+def finish_kernel(field, prof, field_out, prof_out, buffer, sems):
+    halves = 2
+    reads = [pltpu.make_async_copy(field.at[i], buffer.at[i], sems.at[i]) for i in range(halves)]
+    writes = [pltpu.make_async_copy(buffer.at[i], field_out.at[i], sems.at[2 + i]) for i in range(halves)]
+    for read in reads:
+        read.start()
+    prof_out[...] = prof[...]
+    for read, write in zip(reads, writes):
+        read.wait()
+        write.start()
+    for write in writes:
+        write.wait()
+
+
+def finish(field, prof):
+    any_spec = pl.BlockSpec(memory_space=pl.ANY)
+    vmem = pl.BlockSpec(memory_space=pltpu.VMEM)
+    return pl.pallas_call(
+        finish_kernel,
+        out_shape=(
+            jax.ShapeDtypeStruct(field.shape, F32),
+            jax.ShapeDtypeStruct(prof.shape, F32),
+        ),
+        in_specs=[any_spec, vmem],
+        out_specs=(any_spec, vmem),
+        scratch_shapes=[pltpu.VMEM(field.shape, F32), pltpu.SemaphoreType.DMA((4,))],
+        name="finish",
+    )(field, prof)
 
 
 def per_device(phase):
@@ -450,13 +506,11 @@
     height, width = phase.shape
     tiles = width // LANES
     consts = [jnp.asarray(t) for t in tables()]
-    stages = max(1, int(math.log2(n)) - 1)
-    group = 8
-    far = n // group - 1
+    stages = int(math.log2(n)) - 2
     chunks = len(PHASE_ENDS)
     dma = pltpu.SemaphoreType.DMA
     any_spec = pl.BlockSpec(memory_space=pl.ANY)
-    return pl.pallas_call(
+    results = pl.pallas_call(
         functools.partial(kernel, n, tiles),
         out_shape=(
             jax.ShapeDtypeStruct((2, height, width), F32),
@@ -474,9 +528,8 @@
             pltpu.VMEM((2 * WIN, LANES), F32),
             pltpu.VMEM((2, height, width), F32),
             pltpu.VMEM((1, LANES), F32),
+            pltpu.VMEM((n, 1, LANES), F32),
             pltpu.VMEM((1, LANES), F32),
-            pltpu.VMEM((group - 1, 1, LANES), F32),
-            pltpu.VMEM((far, 1, LANES), F32),
             dma((6,)),
             dma((chunks,)),
             dma((chunks,)),
@@ -484,10 +537,10 @@
             dma((ITERS, chunks)),
             dma((ITERS, chunks)),
             dma((ITERS, chunks)),
-            dma((group - 1,)),
-            dma((group - 1,)),
-            dma((far,)),
-            dma((far,)),
+            dma((ROOTS,)),
+            dma,
+            dma((n // ROOTS - 1,)),
+            dma,
             dma,
             pltpu.SemaphoreType.REGULAR((stages,)),
         ],
@@ -496,6 +549,7 @@
         ),
         name="goldstein",
     )(phase, *consts)
+    return finish(*results)
 
 
 def solution(mesh):

time: 59.1 us -> 55.9 us (0.946)
  local copies, waits for them, and re-layouts: 2.25 us -> 0 us
  Pallas kernels: 56.1 us -> 55.1 us
    pallas_call x1, Pallas kernels: 56.1 us -> 52.2 us  [per_device(): pl.pallas_call(functools.partial(kernel, n, tiles), out_shape=(jax.ShapeD...]
    pallas_call x0 -> x1, Pallas kernels: none -> 2.9 us  [finish(): pl.pallas_call(finish_kernel, out_shape=(jax.ShapeDtypeStruct(field.shape...]
    unnamed x4 -> x0, local copies, waits for them, and re-layouts: 2.25 us -> none
where the time goes in v2:
time: 55.9 us; the launch traced here: 55.8 us
  Pallas kernels  55.1 us (99%)
  between operations  0.64 us (1%)
    pallas_call x1, Pallas kernels, per_device(): pl.pallas_call(functools.partial(kernel, n, tiles), out_shape=(jax.ShapeD...  52.2 us
    pallas_call x1, Pallas kernels, finish(): pl.pallas_call(finish_kernel, out_shape=(jax.ShapeDtypeStruct(field.shape...  2.9 us

profile of v2, /device:TPU:37, one launch (start us, length us, event | category | flops | bytes accessed | tf_op | source)
XLA Modules:
  0.0 55.8 jit_solution(5709595724352770314)
XLA Ops:
  0.6 52.2 %goldstein.1 = (f32[2,16,2048]{2,1,0:T(8,128)}, f32[3,16]{1,0:T(4,128)}) custom-call(f32[16,2048]{1,0:T(8,128)} %phase_hbm.1, bf16[64,192]{1,0:T(8,128)(2,1)} %constant.10.clone.row_in_hbm, bf16[768,256]{1,0:T(8,128)(2,1)} %constant.11.clone.col_in_hbm, bf16[768,256]{1,0:T(8,128)(2,1)} %constant.12.clone.col_out_hbm, ...), custom_call_target="tpu_custom_call" | custom-call | tf_op jit(solution)/shard_map/goldstein/pallas_call | solution.py:513
  52.9 2.9 %finish.1 = (f32[2,16,2048]{2,1,0:T(8,128)}, f32[3,16]{1,0:T(4,128)}) custom-call(f32[2,16,2048]{2,1,0:T(8,128)} %get-tuple-element.4.field, f32[3,16]{1,0:T(4,128)} %get-tuple-element.5.prof), custom_call_target="tpu_custom_call" | custom-call | tf_op jit(solution)/shard_map/finish/pallas_call | solution.py:491

commit v3 on v2

--- a/solution.py
+++ b/solution.py
@@ -112,7 +112,7 @@
     col_out_hbm,
     row_out_hbm,
     ones_hbm,
-    out_hbm,
+    out_ref,
     prof_ref,
     phase,
     row_in,
@@ -124,7 +124,6 @@
     eo,
     rv,
     carry,
-    zout,
     pay,
     got,
     answer,
@@ -139,7 +138,6 @@
     pay_recv,
     ans_send,
     ans_recv,
-    out_sem,
     relay,
 ):
     me = lax.axis_index("rows")
@@ -427,11 +425,8 @@
             dn_copy(last, c).wait_send()
 
         final = to_lanes(eo[last, 0, lo:hi] + rv[last, 0, lo:hi])
-        zout[0, :, lo * LANES : hi * LANES] = final[0:HALF]
-        zout[1, :, lo * LANES : hi * LANES] = final[HALF:]
-    store = pltpu.make_async_copy(zout, out_hbm, out_sem)
-    store.start()
-    store.wait()
+        out_ref[0, :, lo * LANES : hi * LANES] = final[0:HALF]
+        out_ref[1, :, lo * LANES : hi * LANES] = final[HALF:]
     for root in range(ROOTS):
 
         @pl.when(me != root)
@@ -471,36 +466,6 @@
             answer_copy(i).wait_send()
 
 
-def finish_kernel(field, prof, field_out, prof_out, buffer, sems):
-    halves = 2
-    reads = [pltpu.make_async_copy(field.at[i], buffer.at[i], sems.at[i]) for i in range(halves)]
-    writes = [pltpu.make_async_copy(buffer.at[i], field_out.at[i], sems.at[2 + i]) for i in range(halves)]
-    for read in reads:
-        read.start()
-    prof_out[...] = prof[...]
-    for read, write in zip(reads, writes):
-        read.wait()
-        write.start()
-    for write in writes:
-        write.wait()
-
-
-def finish(field, prof):
-    any_spec = pl.BlockSpec(memory_space=pl.ANY)
-    vmem = pl.BlockSpec(memory_space=pltpu.VMEM)
-    return pl.pallas_call(
-        finish_kernel,
-        out_shape=(
-            jax.ShapeDtypeStruct(field.shape, F32),
-            jax.ShapeDtypeStruct(prof.shape, F32),
-        ),
-        in_specs=[any_spec, vmem],
-        out_specs=(any_spec, vmem),
-        scratch_shapes=[pltpu.VMEM(field.shape, F32), pltpu.SemaphoreType.DMA((4,))],
-        name="finish",
-    )(field, prof)
-
-
 def per_device(phase):
     n = lax.axis_size("rows")
     height, width = phase.shape
@@ -510,14 +475,14 @@
     chunks = len(PHASE_ENDS)
     dma = pltpu.SemaphoreType.DMA
     any_spec = pl.BlockSpec(memory_space=pl.ANY)
-    results = pl.pallas_call(
+    return pl.pallas_call(
         functools.partial(kernel, n, tiles),
         out_shape=(
-            jax.ShapeDtypeStruct((2, height, width), F32),
-            jax.ShapeDtypeStruct((ITERS, tiles), F32),
+            pltpu.VMEM((2, height, width), F32),
+            pltpu.VMEM((ITERS, tiles), F32),
         ),
         in_specs=[any_spec] * 6,
-        out_specs=(any_spec, pl.BlockSpec(memory_space=pltpu.VMEM)),
+        out_specs=(pl.BlockSpec(memory_space=pltpu.VMEM), pl.BlockSpec(memory_space=pltpu.VMEM)),
         scratch_shapes=[
             pltpu.VMEM((2, height, width), F32),
             *[pltpu.VMEM(c.shape, c.dtype) for c in consts[:4]],
@@ -526,7 +491,6 @@
             pltpu.VMEM((ITERS, 2, tiles, WIN, LANES), F32),
             pltpu.VMEM((ITERS, 2, tiles, WIN, LANES), F32),
             pltpu.VMEM((2 * WIN, LANES), F32),
-            pltpu.VMEM((2, height, width), F32),
             pltpu.VMEM((1, LANES), F32),
             pltpu.VMEM((n, 1, LANES), F32),
             pltpu.VMEM((1, LANES), F32),
@@ -541,7 +505,6 @@
             dma,
             dma((n // ROOTS - 1,)),
             dma,
-            dma,
             pltpu.SemaphoreType.REGULAR((stages,)),
         ],
         compiler_params=pltpu.CompilerParams(
@@ -549,7 +512,6 @@
         ),
         name="goldstein",
     )(phase, *consts)
-    return finish(*results)
 
 
 def solution(mesh):

time: 55.9 us -> 53.7 us (0.961)
  Pallas kernels: 55.1 us -> 51.6 us
  local copies, waits for them, and re-layouts: 0 us -> 1.28 us
    pallas_call x2 -> x1, Pallas kernels: 55.1 us -> 51.6 us  [per_device(): pl.pallas_call(functools.partial(kernel, n, tiles), out_shape=(pltpu.VMEM...]
    unnamed x0 -> x2, local copies, waits for them, and re-layouts: none -> 1.28 us
where the time goes in v3:
time: 53.7 us; the launch traced here: 53.6 us
  Pallas kernels  51.6 us (96%)
  local copies, waits for them, and re-layouts  1.28 us (2%)
  between operations  0.64 us (1%)
    pallas_call x1, Pallas kernels, per_device(): pl.pallas_call(functools.partial(kernel, n, tiles), out_shape=(pltpu.VMEM...  51.6 us
    unnamed x2, local copies, waits for them, and re-layouts  1.28 us

profile of v3, /device:TPU:37, one launch (start us, length us, event | category | flops | bytes accessed | tf_op | source)
XLA Modules:
  0.0 53.6 jit_solution(18112737452270282332)
XLA Ops:
  0.6 51.6 %goldstein.1 = (f32[2,16,2048]{2,1,0:T(8,128)S(1)}, f32[3,16]{1,0:T(4,128)S(1)}) custom-call(f32[16,2048]{1,0:T(8,128)} %phase_hbm.1, bf16[64,192]{1,0:T(8,128)(2,1)} %constant.10.clone.row_in_hbm, bf16[768,256]{1,0:T(8,128)(2,1)} %constant.11.clone.col_in_hbm, bf16[768,256]{1,0:T(8,128)(2,1)} %constant.12.clone.col_out_hbm, ...), custom_call_target="tpu_custom_call" | custom-call | tf_op jit(solution)/shard_map/goldstein/pallas_call | solution.py:478
  52.3 0.7 %copy.10 = f32[2,16,2048]{2,1,0:T(8,128)} copy(f32[2,16,2048]{2,1,0:T(8,128)S(1)} %get-tuple-element.2) | data formatting | bytes 524288
  53.0 0.6 %copy.11 = f32[3,16]{1,0:T(4,128)} copy(f32[3,16]{1,0:T(4,128)S(1)} %get-tuple-element.3) | data formatting | bytes 384

commit v4 on v3

--- a/solution.py
+++ b/solution.py
@@ -260,10 +260,6 @@
         if it == 0:
             lo, hi = (PHASE_ENDS[c - 1] if c else 0), PHASE_ENDS[c]
 
-            @pl.when(has_above)
-            def _():
-                phase_copy(c).wait_send()
-
             @pl.when(has_below)
             def _():
                 phase_copy(c).wait_recv()
@@ -274,13 +270,11 @@
 
         @pl.when(has_above)
         def _():
-            up_copy(it - 1, c).wait_send()
             dn_copy(it - 1, c).wait_recv()
 
         @pl.when(has_below)
         def _():
             up_copy(it - 1, c).wait_recv()
-            dn_copy(it - 1, c).wait_send()
 
         x[lo:hi] = jnp.concatenate(
             [eo[it - 1, 0, lo:hi] + rv[it - 1, 0, lo:hi], eo[it - 1, 1, lo:hi] + rv[it - 1, 1, lo:hi]],
@@ -377,8 +371,8 @@
         for c in range(chunks):
             lo, hi = span(it, c)
             arrive(it, c)
-            if c == 0 and it == 0:
-                relay_step(1)
+            if it == 1 and c == 0:
+                relay_step(2)
             windows(it, lo, hi)
 
             @pl.when(has_above)
@@ -389,17 +383,18 @@
             def _():
                 dn_copy(it, c).start()
 
+            if it == 0 and c == 0:
+                relay_step(1)
         payload = payload + residues(it, 0, tiles)
-        if it == 0:
-            relay_step(2)
 
     last = ITERS - 1
     for c in range(chunks):
+        if c == chunks - 1:
+            for s in range(3, stages):
+                relay_step(s)
         arrive(last, c)
         payload = payload + residues(last, *span(last, c))
     pay[...] = jnp.sum(payload, axis=0, keepdims=True)
-    for s in range(3, stages):
-        relay_step(s)
     for root in range(ROOTS):
 
         @pl.when(me != root)
@@ -420,13 +415,22 @@
         def _():
             dn_copy(last, c).wait_recv()
 
-        @pl.when(has_below)
-        def _():
-            dn_copy(last, c).wait_send()
-
         final = to_lanes(eo[last, 0, lo:hi] + rv[last, 0, lo:hi])
         out_ref[0, :, lo * LANES : hi * LANES] = final[0:HALF]
         out_ref[1, :, lo * LANES : hi * LANES] = final[HALF:]
+    @pl.when(has_above)
+    def _():
+        for c in range(chunks):
+            phase_copy(c).wait_send()
+            for it in range(last):
+                up_copy(it, c).wait_send()
+
+    @pl.when(has_below)
+    def _():
+        for it in range(ITERS):
+            for c in range(chunks):
+                dn_copy(it, c).wait_send()
+
     for root in range(ROOTS):
 
         @pl.when(me != root)
@@ -466,6 +470,33 @@
             answer_copy(i).wait_send()
 
 
+def finish_kernel(field, prof, field_out, prof_out, sems):
+    copies = [
+        pltpu.make_async_copy(field, field_out, sems.at[0]),
+        pltpu.make_async_copy(prof, prof_out, sems.at[1]),
+    ]
+    for copy in copies:
+        copy.start()
+    for copy in copies:
+        copy.wait()
+
+
+def finish(field, prof):
+    any_spec = pl.BlockSpec(memory_space=pl.ANY)
+    vmem = pl.BlockSpec(memory_space=pltpu.VMEM)
+    return pl.pallas_call(
+        finish_kernel,
+        out_shape=(
+            jax.ShapeDtypeStruct(field.shape, F32),
+            jax.ShapeDtypeStruct(prof.shape, F32),
+        ),
+        in_specs=[vmem, vmem],
+        out_specs=(any_spec, any_spec),
+        scratch_shapes=[pltpu.SemaphoreType.DMA((2,))],
+        name="finish",
+    )(field, prof)
+
+
 def per_device(phase):
     n = lax.axis_size("rows")
     height, width = phase.shape
@@ -475,7 +506,7 @@
     chunks = len(PHASE_ENDS)
     dma = pltpu.SemaphoreType.DMA
     any_spec = pl.BlockSpec(memory_space=pl.ANY)
-    return pl.pallas_call(
+    results = pl.pallas_call(
         functools.partial(kernel, n, tiles),
         out_shape=(
             pltpu.VMEM((2, height, width), F32),
@@ -512,6 +543,7 @@
         ),
         name="goldstein",
     )(phase, *consts)
+    return finish(*[pltpu.with_memory_space_constraint(r, pltpu.VMEM) for r in results])
 
 
 def solution(mesh):

time: 53.7 us -> 53 us (0.987)
  local copies, waits for them, and re-layouts: 1.28 us -> 0 us
  Pallas kernels: 51.6 us -> 52.3 us
    unnamed x2 -> x0, local copies, waits for them, and re-layouts: 1.28 us -> none
    pallas_call x0 -> x1, Pallas kernels: none -> 0.72 us  [finish(): pl.pallas_call(finish_kernel, out_shape=(jax.ShapeDtypeStruct(field.shape...]
where the time goes in v4:
time: 53 us; the launch traced here: 52.9 us
  Pallas kernels  52.3 us (99%)
  between operations  0.64 us (1%)
    pallas_call x1, Pallas kernels, per_device(): pl.pallas_call(functools.partial(kernel, n, tiles), out_shape=(pltpu.VMEM...  51.5 us

profile of v4, /device:TPU:37, one launch (start us, length us, event | category | flops | bytes accessed | tf_op | source)
XLA Modules:
  0.0 52.9 jit_solution(6541992363408629869)
XLA Ops:
  0.6 51.5 %goldstein.1 = (f32[2,16,2048]{2,1,0:T(8,128)S(1)}, f32[3,16]{1,0:T(4,128)S(1)}) custom-call(f32[16,2048]{1,0:T(8,128)} %phase_hbm.1, bf16[64,192]{1,0:T(8,128)(2,1)} %constant.10.clone.row_in_hbm, bf16[768,256]{1,0:T(8,128)(2,1)} %constant.11.clone.col_in_hbm, bf16[768,256]{1,0:T(8,128)(2,1)} %constant.12.clone.col_out_hbm, ...), custom_call_target="tpu_custom_call" | custom-call | tf_op jit(solution)/shard_map/goldstein/pallas_call | solution.py:509
  52.2 0.7 %finish.1 = (f32[2,16,2048]{2,1,0:T(8,128)}, f32[3,16]{1,0:T(4,128)}) custom-call(f32[2,16,2048]{2,1,0:T(8,128)S(1)} %get-tuple-element.4.field, f32[3,16]{1,0:T(4,128)S(1)} %get-tuple-element.5.prof), custom_call_target="tpu_custom_call" | custom-call | tf_op jit(solution)/shard_map/finish/pallas_call | solution.py:487

commit v5 on v4

--- a/solution.py
+++ b/solution.py
@@ -17,7 +17,8 @@
 F32 = jnp.float32
 BF16 = jnp.bfloat16
 MESH = pl.DeviceIdType.MESH
-ROOTS = 4
+ROOTS = 8
+TELLERS = 4
 
 PHASE_ENDS = (7, 12, 16)
 CHUNK_ENDS = ((6, 11, 16), (5, 10, 16), (4, 9, 16))
@@ -201,7 +202,7 @@
         return pltpu.make_async_remote_copy(
             src_ref=phase.at[0, :, cols],
             dst_ref=phase.at[1, :, cols],
-            send_sem=ph_send.at[c],
+            send_sem=ph_send,
             recv_sem=ph_recv.at[c],
             device_id={"rows": jnp.maximum(me - 1, 0)},
             device_id_type=MESH,
@@ -216,7 +217,7 @@
         return pltpu.make_async_remote_copy(
             src_ref=eo.at[it, 0, pl.ds(lo, hi - lo)],
             dst_ref=rv.at[it, 1, pl.ds(lo, hi - lo)],
-            send_sem=up_send.at[it, c],
+            send_sem=up_send,
             recv_sem=up_recv.at[it, c],
             device_id={"rows": jnp.maximum(me - 1, 0)},
             device_id_type=MESH,
@@ -227,7 +228,7 @@
         return pltpu.make_async_remote_copy(
             src_ref=eo.at[it, 1, pl.ds(lo, hi - lo)],
             dst_ref=rv.at[it, 0, pl.ds(lo, hi - lo)],
-            send_sem=dn_send.at[it, c],
+            send_sem=dn_send,
             recv_sem=dn_recv.at[it, c],
             device_id={"rows": jnp.minimum(me + 1, n - 1)},
             device_id_type=MESH,
@@ -348,7 +349,7 @@
         return pltpu.make_async_remote_copy(
             src_ref=pay,
             dst_ref=got.at[lax.rem(me - root + n, n)],
-            send_sem=pay_send.at[root],
+            send_sem=pay_send,
             recv_sem=pay_recv,
             device_id={"rows": root},
             device_id_type=MESH,
@@ -358,9 +359,9 @@
         return pltpu.make_async_remote_copy(
             src_ref=answer,
             dst_ref=answer,
-            send_sem=ans_send.at[i],
+            send_sem=ans_send,
             recv_sem=ans_recv,
-            device_id={"rows": jnp.minimum(me + ROOTS * (i + 1), n - 1)},
+            device_id={"rows": jnp.minimum(me + TELLERS * (i + 1), n - 1)},
             device_id_type=MESH,
         )
 
@@ -418,56 +419,61 @@
         final = to_lanes(eo[last, 0, lo:hi] + rv[last, 0, lo:hi])
         out_ref[0, :, lo * LANES : hi * LANES] = final[0:HALF]
         out_ref[1, :, lo * LANES : hi * LANES] = final[HALF:]
+    def sent(ref, sem):
+        pltpu.make_async_remote_copy(
+            src_ref=ref,
+            dst_ref=ref,
+            send_sem=sem,
+            recv_sem=pay_recv,
+            device_id=ring(1),
+            device_id_type=MESH,
+        ).wait_send()
+
     @pl.when(has_above)
     def _():
-        for c in range(chunks):
-            phase_copy(c).wait_send()
-            for it in range(last):
-                up_copy(it, c).wait_send()
+        sent(phase.at[0], ph_send)
+        sent(eo.at[pl.ds(0, last), 0], up_send)
 
     @pl.when(has_below)
     def _():
-        for it in range(ITERS):
-            for c in range(chunks):
-                dn_copy(it, c).wait_send()
-
-    for root in range(ROOTS):
-
-        @pl.when(me != root)
-        def _():
-            pay_copy(root).wait_send()
+        sent(eo.at[pl.ds(0, ITERS), 1], dn_send)
 
     is_root = me < ROOTS
-    answers = ans_send.shape[0]
+    is_teller = jnp.logical_and(is_root, me >= ROOTS - TELLERS)
+    answers = (n - ROOTS) // TELLERS
 
     @pl.when(is_root)
     def _():
+        sent(got.at[pl.ds(0, ROOTS - 1)], pay_send)
         others = got.at[pl.ds(1, n - 1)]
         pltpu.make_async_remote_copy(
             src_ref=others,
             dst_ref=others,
-            send_sem=pay_send.at[0],
+            send_sem=pay_send,
             recv_sem=pay_recv,
             device_id=ring(1),
             device_id_type=MESH,
         ).wait_recv()
         total = pay[...] + jnp.sum(got[1:n], axis=0)
         answer[...] = total * (1.0 / (n * HALF * LANES))
+
+    @pl.when(is_teller)
+    def _():
         for i in range(answers):
             answer_copy(i).start()
 
     @pl.when(jnp.logical_not(is_root))
     def _():
+        sent(got.at[pl.ds(0, ROOTS)], pay_send)
         answer_copy(0).wait_recv()
 
     for it in range(ITERS):
         moved = answer[...] if it == 0 else pltpu.roll(answer[...], LANES - it * tiles, 1)
         prof_ref[it : it + 1, :] = moved[:, 0:tiles]
 
-    @pl.when(is_root)
-    def _():
-        for i in range(answers):
-            answer_copy(i).wait_send()
+    @pl.when(is_teller)
+    def _():
+        sent(got.at[pl.ds(0, answers)], ans_send)
 
 
 def finish_kernel(field, prof, field_out, prof_out, sems):
@@ -526,15 +532,15 @@
             pltpu.VMEM((n, 1, LANES), F32),
             pltpu.VMEM((1, LANES), F32),
             dma((6,)),
+            dma,
             dma((chunks,)),
-            dma((chunks,)),
+            dma,
             dma((ITERS, chunks)),
+            dma,
             dma((ITERS, chunks)),
-            dma((ITERS, chunks)),
-            dma((ITERS, chunks)),
-            dma((ROOTS,)),
-            dma,
-            dma((n // ROOTS - 1,)),
+            dma,
+            dma,
+            dma,
             dma,
             pltpu.SemaphoreType.REGULAR((stages,)),
         ],

time: 53 us -> 51.8 us (0.977)
  Pallas kernels: 52.3 us -> 51 us
    pallas_call x1, Pallas kernels: 51.5 us -> 50.3 us  [per_device(): pl.pallas_call(functools.partial(kernel, n, tiles), out_shape=(pltpu.VMEM...]
where the time goes in v5:
time: 51.8 us; the launch traced here: 51.7 us
  Pallas kernels  51 us (98%)
  between operations  0.64 us (1%)
    pallas_call x1, Pallas kernels, per_device(): pl.pallas_call(functools.partial(kernel, n, tiles), out_shape=(pltpu.VMEM...  50.3 us

profile of v5, /device:TPU:37, one launch (start us, length us, event | category | flops | bytes accessed | tf_op | source)
XLA Modules:
  0.0 51.7 jit_solution(6375327934765157830)
XLA Ops:
  0.6 50.3 %goldstein.1 = (f32[2,16,2048]{2,1,0:T(8,128)S(1)}, f32[3,16]{1,0:T(4,128)S(1)}) custom-call(f32[16,2048]{1,0:T(8,128)} %phase_hbm.1, bf16[64,192]{1,0:T(8,128)(2,1)} %constant.10.clone.row_in_hbm, bf16[768,256]{1,0:T(8,128)(2,1)} %constant.11.clone.col_in_hbm, bf16[768,256]{1,0:T(8,128)(2,1)} %constant.12.clone.col_out_hbm, ...), custom_call_target="tpu_custom_call" | custom-call | tf_op jit(solution)/shard_map/goldstein/pallas_call | solution.py:515
  51.0 0.7 %finish.1 = (f32[2,16,2048]{2,1,0:T(8,128)}, f32[3,16]{1,0:T(4,128)}) custom-call(f32[2,16,2048]{2,1,0:T(8,128)S(1)} %get-tuple-element.4.field, f32[3,16]{1,0:T(4,128)S(1)} %get-tuple-element.5.prof), custom_call_target="tpu_custom_call" | custom-call | tf_op jit(solution)/shard_map/finish/pallas_call | solution.py:493

commit v6 on v5

--- a/solution.py
+++ b/solution.py
@@ -79,6 +79,13 @@
 
 def dot(a, b):
     return jnp.dot(a, b, preferred_element_type=F32)
+
+
+def halves(x, table):
+    half = x.shape[0] // 2
+    return jnp.concatenate(
+        [dot(split_cols(x[:half]), table[...]), dot(split_cols(x[half:]), table[...])], axis=0
+    )
 
 
 def unit(phase):
@@ -326,11 +333,11 @@
 
         y = both(y)
         y = jnp.concatenate([y[:, 0:WIN], y[:, WIN:]], axis=2).reshape(2 * count * WIN, 2 * LANES)
-        s = dot(split_cols(y), col_in[...]).reshape(2 * count, WIN, 2 * LANES)
+        s = halves(y, col_in).reshape(2 * count, WIN, 2 * LANES)
         sr, si = s[:, :, 0:LANES], s[:, :, LANES:]
         gain = lax.rsqrt(lax.rsqrt((sr * sr + si * si) * inverse))
         s = jnp.concatenate([sr * gain, si * gain], axis=2).reshape(2 * count * WIN, 2 * LANES)
-        s = dot(split_cols(s), col_out[...]).reshape(2 * count, WIN, 2 * LANES)
+        s = halves(s, col_out).reshape(2 * count, WIN, 2 * LANES)
         s = jnp.concatenate([s[:, :, 0:LANES], s[:, :, LANES:]], axis=1)
         moved = pltpu.roll(s[count:], HALF, 2)
         if lo == 0:

time: 51.8 us -> 51.1 us (0.986)
  Pallas kernels: 51 us -> 50.3 us
    pallas_call x1, Pallas kernels: 50.3 us -> 49.6 us  [per_device(): pl.pallas_call(functools.partial(kernel, n, tiles), out_shape=(pltpu.VMEM...]
where the time goes in v6:
time: 51.1 us; the launch traced here: 51 us
  Pallas kernels  50.3 us (98%)
  between operations  0.64 us (1%)
    pallas_call x1, Pallas kernels, per_device(): pl.pallas_call(functools.partial(kernel, n, tiles), out_shape=(pltpu.VMEM...  49.6 us

profile of v6, /device:TPU:37, one launch (start us, length us, event | category | flops | bytes accessed | tf_op | source)
XLA Modules:
  0.0 51.0 jit_solution(8719572456796735030)
XLA Ops:
  0.6 49.6 %goldstein.1 = (f32[2,16,2048]{2,1,0:T(8,128)S(1)}, f32[3,16]{1,0:T(4,128)S(1)}) custom-call(f32[16,2048]{1,0:T(8,128)} %phase_hbm.1, bf16[64,192]{1,0:T(8,128)(2,1)} %constant.10.clone.row_in_hbm, bf16[768,256]{1,0:T(8,128)(2,1)} %constant.11.clone.col_in_hbm, bf16[768,256]{1,0:T(8,128)(2,1)} %constant.12.clone.col_out_hbm, ...), custom_call_target="tpu_custom_call" | custom-call | tf_op jit(solution)/shard_map/goldstein/pallas_call | solution.py:522
  50.2 0.7 %finish.1 = (f32[2,16,2048]{2,1,0:T(8,128)}, f32[3,16]{1,0:T(4,128)}) custom-call(f32[2,16,2048]{2,1,0:T(8,128)S(1)} %get-tuple-element.4.field, f32[3,16]{1,0:T(4,128)S(1)} %get-tuple-element.5.prof), custom_call_target="tpu_custom_call" | custom-call | tf_op jit(solution)/shard_map/finish/pallas_call | solution.py:500

commit v7 on v6

--- a/solution.py
+++ b/solution.py
@@ -11,6 +11,7 @@
 
 ITERS = 3
 EPS = 1e-06
+TINY = float(np.finfo(np.float32).tiny)
 WIN = 32
 HALF = 16
 LANES = 128
@@ -335,7 +336,8 @@
         y = jnp.concatenate([y[:, 0:WIN], y[:, WIN:]], axis=2).reshape(2 * count * WIN, 2 * LANES)
         s = halves(y, col_in).reshape(2 * count, WIN, 2 * LANES)
         sr, si = s[:, :, 0:LANES], s[:, :, LANES:]
-        gain = lax.rsqrt(lax.rsqrt((sr * sr + si * si) * inverse))
+        ratio = jnp.maximum((sr * sr + si * si) * inverse, TINY)
+        gain = lax.rsqrt(lax.rsqrt(ratio))
         s = jnp.concatenate([sr * gain, si * gain], axis=2).reshape(2 * count * WIN, 2 * LANES)
         s = halves(s, col_out).reshape(2 * count, WIN, 2 * LANES)
         s = jnp.concatenate([s[:, :, 0:LANES], s[:, :, LANES:]], axis=1)

time: 51.1 us -> 51.1 us (level)
  no operation moved by 1% of the time
where the time goes in v7:
time: 51.1 us; the launch traced here: 51 us
  Pallas kernels  50.3 us (98%)
  between operations  0.64 us (1%)
    pallas_call x1, Pallas kernels, per_device(): pl.pallas_call(functools.partial(kernel, n, tiles), out_shape=(pltpu.VMEM...  49.6 us

profile of v7, /device:TPU:37, one launch (start us, length us, event | category | flops | bytes accessed | tf_op | source)
XLA Modules:
  0.0 51.0 jit_solution(9898728150811142109)
XLA Ops:
  0.6 49.6 %goldstein.1 = (f32[2,16,2048]{2,1,0:T(8,128)S(1)}, f32[3,16]{1,0:T(4,128)S(1)}) custom-call(f32[16,2048]{1,0:T(8,128)} %phase_hbm.1, bf16[64,192]{1,0:T(8,128)(2,1)} %constant.10.clone.row_in_hbm, bf16[768,256]{1,0:T(8,128)(2,1)} %constant.11.clone.col_in_hbm, bf16[768,256]{1,0:T(8,128)(2,1)} %constant.12.clone.col_out_hbm, ...), custom_call_target="tpu_custom_call" | custom-call | tf_op jit(solution)/shard_map/goldstein/pallas_call | solution.py:524
  50.2 0.7 %finish.1 = (f32[2,16,2048]{2,1,0:T(8,128)}, f32[3,16]{1,0:T(4,128)}) custom-call(f32[2,16,2048]{2,1,0:T(8,128)S(1)} %get-tuple-element.4.field, f32[3,16]{1,0:T(4,128)S(1)} %get-tuple-element.5.prof), custom_call_target="tpu_custom_call" | custom-call | tf_op jit(solution)/shard_map/finish/pallas_call | solution.py:502
